TPU v7x, 256 devices: a 8x8x2 block of a 8x8x16 slice. The times are simulated.
256 devices in a mesh: parts: 2 (over z), tok: 64 (over x, y), sub: 2 (over core).
Axes of the slice: x: 8, y: 8, z: 2, core: 2. Of those that a mesh axis runs over, the one named last changes fastest.
The devices are a block of a 8x8x16 slice.
Arguments:
- video: bfloat16 [16, 48, 128, 768], P('parts', None, ('tok', 'sub')), parts along dimension 0, may hold values from -6 to 6
- norm_gain: float32 [3, 768], replicated, may hold values from 0.1 to 1.9
- qkv_weight: bfloat16 [3, 3, 768, 768], P(None, None, None, 'sub'), may hold values from -0.21875 to 0.21875
- out_weight: bfloat16 [3, 768, 768], P(None, 'sub'), may hold values from -0.21875 to 0.21875
Outputs:
- refined: bfloat16 [16, 48, 128, 768], P('parts', None, ('tok', 'sub')), parts along dimension 0
There are 2 independent parts, one for each index of `parts`. A program takes and returns all parts, laid end to end along the dimension named above; an argument that names none is the same for every part. Nothing has to cross between parts.
All inputs are finite; a program needn't handle non-finite values.
Results may differ from a plain program's by a relative error of at most 0.014.
Values may be sent and summed in bfloat16 or wider, within the bound.
A program may use at most 64 MiB of HBM per device.

v0:
```python
import functools
import math

import jax
import jax.numpy as jnp
from jax import lax
from jax.experimental import pallas as pl
from jax.experimental.pallas import tpu as pltpu
from jax.sharding import PartitionSpec as P

HEAD_DIM = 64
EPSILON = 1e-06
PAIR = 2 * HEAD_DIM
MESH = pl.DeviceIdType.MESH
F32, BF16 = jnp.float32, jnp.bfloat16
CROSS = (((1,), (1,)), ((), ()))


def iota(shape, dim):
    return lax.broadcasted_iota(jnp.int32, shape, dim)


def one_hot(condition):
    return jnp.where(condition, 1.0, 0.0).astype(BF16)


def matmul(a, b):
    return jnp.dot(a, b, preferred_element_type=F32)


def kernel(side, video_hbm, gain_ref, wqkv_hbm, wo_hbm, out_ref,
           x0, x1, x2, normed, qkv, mixed, wqkv, wo,
           sa1, sb1, ra1, rb1, sa2, sb2, ra2, rb2,
           ta1, tb1, ua1, ub1, ta2, tb2, ub2,
           local_sem, wsend, wrecv, ssem, rsem):
    frames, rows, width = x0.shape
    half = width // 2
    pairs = half // PAIR
    chunks = ra1.shape[0]
    band = rows // chunks
    count = frames * band
    tok, s = lax.axis_index("tok"), lax.axis_index("sub")
    o = 1 - s
    gx, gy = tok // side, lax.rem(tok, side)
    slot_x, slot_y = gx * 2 + s, gy * 2 + s

    def other(g, k):
        return lax.rem(g + k, side)

    def at_x(g, core):
        return {"tok": g * side + gy, "sub": core}

    def at_y(g, core):
        return {"tok": gx * side + g, "sub": core}

    i, j = iota((count, count), 0), iota((count, count), 1)
    two = 2 * side
    swap_lines = one_hot(j == lax.rem(i // 2, side) * two + (i // two) * 2 + lax.rem(i, 2))
    group = one_hot(j == lax.rem(i, side) * two + i // side)
    ungroup = one_hot(j == lax.rem(i, two) * side + i // two)
    swap_tokens = one_hot(j == lax.rem(i, side) * two + lax.rem(i // side, 2) * side + i // two)

    load_x = pltpu.make_async_copy(video_hbm, x0, local_sem.at[0])
    load_x.start()

    def load_w(l):
        return (pltpu.make_async_copy(wqkv_hbm.at[l], wqkv.at[l, s], local_sem.at[1 + 2 * l]),
                pltpu.make_async_copy(wo_hbm.at[l], wo.at[l, s], local_sem.at[2 + 2 * l]))

    def pass_w(l, part):
        if part < 3:
            return pltpu.make_async_remote_copy(
                wqkv_hbm.at[l, part], wqkv.at[l, s, part], wsend.at[l, part], wrecv.at[l, part],
                device_id={"sub": o}, device_id_type=MESH)
        return pltpu.make_async_remote_copy(
            wo_hbm.at[l], wo.at[l, s], wsend.at[l, 3], wrecv.at[l, 3],
            device_id={"sub": o}, device_id_type=MESH)

    for l in range(3):
        for copy in load_w(l):
            copy.start()
    barrier = pltpu.get_barrier_semaphore()
    pl.semaphore_signal(barrier, inc=1, device_id={"sub": o}, device_id_type=MESH)
    for k in range(1, side):
        for core in range(2):
            pl.semaphore_signal(barrier, inc=1, device_id=at_x(other(gx, k), core), device_id_type=MESH)
            pl.semaphore_signal(barrier, inc=1, device_id=at_y(other(gy, k), core), device_id_type=MESH)

    lane = iota((1, PAIR), 1)
    left, right = one_hot(lane < HEAD_DIM), one_hot(lane >= HEAD_DIM)
    r, c2 = iota((PAIR, PAIR), 0), iota((PAIR, PAIR), 1)
    mean_heads = (jnp.where(r // HEAD_DIM == c2 // HEAD_DIM, 1.0 / HEAD_DIM, 0.0)).astype(BF16)

    def span(c):
        return pl.ds(pl.multiple_of(c * band, band), band)

    def normalize(src, l, c):
        values = src[:, span(c), :].reshape(count, width).astype(F32)
        scale = lax.rsqrt(jnp.mean(values * values, axis=-1, keepdims=True) + EPSILON)
        out = (values * scale * gain_ref[l:l + 1, :]).astype(BF16)
        normed[:, span(c), :] = out.reshape(frames, band, width)

    def project(l, c, h):
        flat = normed[:, span(c), :].reshape(count, width)
        for part in range(3):
            y = matmul(flat, wqkv[l, h, part])
            if part < 2:
                square = (y * y).astype(BF16)
                y = jnp.concatenate([
                    y[:, p * PAIR:(p + 1) * PAIR] * lax.rsqrt(
                        matmul(square[:, p * PAIR:(p + 1) * PAIR], mean_heads) + EPSILON)
                    for p in range(pairs)], axis=1)
            qkv[part, h, :, span(c), :] = y.astype(BF16).reshape(frames, band, half)

    def attend_pair(q, k, v, mask):
        n = q.shape[0]
        kk = jnp.concatenate([k * left, k * right], axis=0)
        scores = lax.dot_general(q, kk, CROSS, preferred_element_type=F32)
        expo = jnp.exp2(scores * (math.log2(math.e) / math.sqrt(HEAD_DIM)))
        if mask is not None:
            expo = expo * mask
        ones = jnp.concatenate([jnp.broadcast_to(left, (n, PAIR)), jnp.broadcast_to(right, (n, PAIR))], axis=0)
        vv = jnp.concatenate([jnp.concatenate([v * left, v * right], axis=0), ones], axis=1)
        both = matmul(expo.astype(BF16), vv)
        return (both[:, :PAIR] / both[:, PAIR:]).astype(BF16)

    def attend(c, h, mask):
        for p in range(pairs):
            lanes = slice(p * PAIR, (p + 1) * PAIR)
            q, k, v = (qkv[part, h, :, span(c), lanes].reshape(count, PAIR) for part in range(3))
            mixed[h, :, span(c), lanes] = attend_pair(q, k, v, mask).reshape(frames, band, PAIR)

    def output(src, l, c):
        total = src[:, span(c), :].reshape(count, width).astype(F32)
        update = (matmul(mixed[0, :, span(c), :].reshape(count, half), wo[l, 0])
                  + matmul(mixed[1, :, span(c), :].reshape(count, half), wo[l, 1]))
        return (total + update).astype(BF16)

    def permute(matrix, values):
        return matmul(matrix, values).astype(BF16)

    order = sorted(range(1, side), key=lambda k: -min(k, side - k))

    def ring(send, recv, sem, c, me, place):
        for k in order:
            g = other(me, k)
            pltpu.make_async_remote_copy(
                send.at[c, g], recv.at[c, me], ssem.at[sem, c], rsem.at[sem, c],
                device_id=place(g, s), device_id_type=MESH).start()
        recv[c, me] = send[c, me]

    def fan(send, recv, sem, c, me, slot, place):
        for k in order:
            g = other(me, k)
            for core in range(2):
                pltpu.make_async_remote_copy(
                    send.at[c, g * 2 + core], recv.at[c, slot], ssem.at[sem, c], rsem.at[sem, c],
                    device_id=place(g, core), device_id_type=MESH).start()
        pltpu.make_async_remote_copy(
            send.at[c, me * 2 + o], recv.at[c, slot], ssem.at[sem, c], rsem.at[sem, c],
            device_id={"sub": o}, device_id_type=MESH).start()
        recv[c, slot] = send[c, slot]

    def arrived(recv, sem, c):
        pieces = recv.at[c, pl.ds(0, recv.shape[1] - 1)]
        pltpu.make_async_copy(pieces, pieces, rsem.at[sem, c]).wait()

    def sent(send, sem, c):
        pieces = send.at[c, pl.ds(0, send.shape[1] - 1)]
        pltpu.make_async_copy(pieces, pieces, ssem.at[sem, c]).wait()

    def flat(recv, c):
        return recv[c].reshape(count, half)

    def start_out(c, values):
        sa1[c] = values[:, :half].reshape(side, two, half)
        sb1[c] = permute(swap_lines, values[:, half:]).reshape(side, two, half)
        ring(sa1, ra1, 0, c, gx, at_x)
        ring(sb1, rb1, 1, c, gy, at_y)

    def relay_out(c):
        arrived(ra1, 0, c)
        sa2[c] = permute(group, flat(ra1, c)).reshape(two, side, half)
        fan(sa2, ra2, 2, c, gy, slot_y, at_y)
        arrived(rb1, 1, c)
        sb2[c] = permute(group, flat(rb1, c)).reshape(two, side, half)
        fan(sb2, rb2, 3, c, gx, slot_x, at_x)

    def finish_out(c):
        arrived(ra2, 2, c)
        x1[:, span(c), 0:half] = flat(ra2, c).reshape(frames, band, half)
        arrived(rb2, 3, c)
        x1[:, span(c), half:width] = permute(swap_tokens, flat(rb2, c)).reshape(frames, band, half)

    def start_back(c, values):
        ta1[c] = values[:, :half].reshape(two, side, half)
        tb1[c] = permute(swap_tokens, values[:, half:]).reshape(two, side, half)
        fan(ta1, ua1, 4, c, gy, slot_y, at_y)
        fan(tb1, ub1, 5, c, gx, slot_x, at_x)

    def relay_back(c):
        arrived(ua1, 4, c)
        ta2[c] = permute(ungroup, flat(ua1, c)).reshape(side, two, half)
        for k in order:
            g = other(gx, k)
            pltpu.make_async_remote_copy(
                ta2.at[c, g], x2.at[gx, span(c), pl.ds(0, half)], ssem.at[6, c], rsem.at[6, c],
                device_id=at_x(g, s), device_id_type=MESH).start()
        x2[gx, span(c), 0:half] = ta2[c, gx]
        arrived(ub1, 5, c)
        tb2[c] = permute(ungroup, flat(ub1, c)).reshape(side, two, half)
        ring(tb2, ub2, 7, c, gy, at_y)

    def finish_back(c):
        sent_like = ta2.at[c, pl.ds(0, side - 1)]
        pltpu.make_async_copy(sent_like, sent_like, rsem.at[6, c]).wait()
        arrived(ub2, 7, c)
        x2[:, span(c), half:width] = permute(swap_lines, flat(ub2, c)).reshape(frames, band, half)

    load_x.wait()
    for copy in load_w(0):
        copy.wait()

    @pl.loop(0, chunks)
    def _(c):
        normalize(x0, 0, c)
        project(0, c, s)

    pl.semaphore_wait(barrier, 4 * (side - 1) + 1)
    for l in range(2):
        for part in range(4):
            pass_w(l, part).start()
    i2, j2 = iota((count, 2 * count), 0), iota((count, 2 * count), 1)
    same_row = jnp.where(lax.rem(i2, band) == lax.rem(j2, band), 1.0, 0.0)

    @pl.loop(0, chunks)
    def _(c):
        attend(c, s, same_row)

    for part in range(3):
        pass_w(0, part).wait_recv()

    @pl.loop(0, chunks)
    def _(c):
        project(0, c, o)
        attend(c, o, same_row)

        @pl.when(c == 0)
        def _():
            pass_w(0, 3).wait_recv()

        start_out(c, output(x0, 0, c))

        @pl.when(c > 0)
        def _():
            relay_out(c - 1)

    relay_out(chunks - 1)
    for part in range(4):
        pass_w(2, part).start()

    for copy in load_w(1):
        copy.wait()
    for part in range(4):
        pass_w(1, part).wait_recv()

    @pl.loop(0, chunks)
    def _(c):
        finish_out(c)
        normalize(x1, 1, c)
        for h in range(2):
            project(1, c, h)
            attend(c, h, None)
        start_back(c, output(x1, 1, c))

        @pl.when(c > 0)
        def _():
            relay_back(c - 1)

    relay_back(chunks - 1)

    for copy in load_w(2):
        copy.wait()
    for part in range(4):
        pass_w(2, part).wait_recv()

    @pl.loop(0, chunks)
    def _(c):
        finish_back(c)
        normalize(x2, 2, c)
        for h in range(2):
            project(2, c, h)

    @pl.loop(0, frames)
    def _(f):
        for h in range(2):
            for p in range(pairs):
                lanes = slice(p * PAIR, (p + 1) * PAIR)
                mixed[h, f, :, lanes] = attend_pair(qkv[0, h, f, :, lanes], qkv[1, h, f, :, lanes], qkv[2, h, f, :, lanes], None)

    @pl.loop(0, chunks)
    def _(c):
        out_ref[:, span(c), :] = output(x2, 2, c).reshape(frames, band, width)

    for l in range(3):
        for part in range(4):
            pass_w(l, part).wait_send()

    @pl.loop(0, chunks)
    def _(c):
        for sem, send in enumerate((sa1, sb1, sa2, sb2, ta1, tb1, ta2, tb2)):
            sent(send, sem, c)


def body(side, video, norm_gain, qkv_weight, out_weight):
    frames, rows, cols, width = video.shape
    half = width // 2
    lines = 2 * side * side
    chunks = frames * rows // lines
    ring = pltpu.VMEM((chunks, side, 2 * side, half), BF16)
    fan = pltpu.VMEM((chunks, 2 * side, side, half), BF16)
    tokens = pltpu.VMEM((frames, rows, width), BF16)
    dma = pltpu.SemaphoreType.DMA
    anywhere = pl.BlockSpec(memory_space=pl.ANY)
    vmem = pl.BlockSpec(memory_space=pltpu.VMEM)
    out = pl.pallas_call(
        functools.partial(kernel, side),
        out_shape=jax.ShapeDtypeStruct((frames, rows, width), BF16),
        in_specs=[anywhere, vmem, anywhere, anywhere],
        out_specs=vmem,
        scratch_shapes=[
            tokens, tokens, tokens, tokens,
            pltpu.VMEM((3, 2, frames, rows, half), BF16),
            pltpu.VMEM((2, frames, rows, half), BF16),
            pltpu.VMEM((3, 2, 3, width, half), BF16),
            pltpu.VMEM((3, 2, half, width), BF16),
            ring, ring, ring, ring, fan, fan, fan, fan,
            fan, fan, fan, fan, ring, ring, ring,
            dma((7,)), dma((3, 4)), dma((3, 4)), dma((8, chunks)), dma((8, chunks)),
        ],
        compiler_params=pltpu.CompilerParams(
            collective_id=0, has_side_effects=True, vmem_limit_bytes=60 * 1024 * 1024),
    )(video.reshape(frames, rows, width), norm_gain, qkv_weight, out_weight)
    return out.reshape(video.shape)


def solution(mesh):
    side = math.isqrt(mesh.shape["tok"])
    in_specs = (
        P("parts", None, ("tok", "sub"), None),
        P(),
        P(None, None, None, "sub"),
        P(None, "sub", None),
    )
    out_specs = P("parts", None, ("tok", "sub"), None)
    return jax.shard_map(functools.partial(body, side), mesh=mesh, in_specs=in_specs, out_specs=out_specs, check_vma=False)
```

profile of v0, /device:TPU:513, one launch (start us, length us, event | category | flops | bytes accessed | tf_op | source)
XLA Modules:
  0.0 78.9 jit_solution(2199996558065483660)
XLA Ops:
  0.0 76.9 %shard_map.46 = bf16[8,48,768]{2,1,0:T(8,128)(2,1)} custom-call(bf16[8,48,768]{2,1,0:T(8,128)(2,1)} %bitcast.5, f32[3,768]{1,0:T(4,128)} %gain_ref.1, bf16[3,3,768,384]{3,2,1,0:T(8,128)(2,1)} %wqkv_hbm.1, bf16[3,384,768]{2,1,0:T(8,128)(2,1)} %wo_hbm.1), custom_call_target="tpu_custom_call" | custom-call | tf_op jit(solution)/shard_map/pallas_call | solution.py:326
  77.0 1.9 %copy.7 = bf16[8,48,1,768]{3,1,2,0:T(8,128)(2,1)} copy(bf16[8,48,1,768]{3,1,2,0:T(8,128)(2,1)} %bitcast.4) | data formatting | bytes 1179648
where the time goes:
time: 79.1 us; the launch traced here: 78.9 us
  Pallas kernels  76.9 us (97%)
  local copies, waits for them, and re-layouts  1.92 us (2%)
    pallas_call x1, Pallas kernels, body(): pl.pallas_call(functools.partial(kernel, side), out_shape=jax.ShapeDtypeS...  76.9 us
    unnamed x1, local copies, waits for them, and re-layouts  1.92 us

commit v1 on v0

v1 whole, which is shorter than its diff:
```python
import functools
import math

import jax
import jax.numpy as jnp
from jax import lax
from jax.experimental import pallas as pl
from jax.experimental.pallas import tpu as pltpu
from jax.sharding import PartitionSpec as P

HEAD_DIM = 64
EPSILON = 1e-06
PAIR = 2 * HEAD_DIM
MESH = pl.DeviceIdType.MESH
F32, BF16 = jnp.float32, jnp.bfloat16
CROSS = (((1,), (1,)), ((), ()))


def iota(shape, dim):
    return lax.broadcasted_iota(jnp.int32, shape, dim)


def one_hot(condition):
    return jnp.where(condition, 1.0, 0.0).astype(BF16)


def matmul(a, b):
    return jnp.dot(a, b, preferred_element_type=F32)


def kernel(side, video_hbm, gain_ref, wqkv_hbm, wo_hbm, out_ref,
           x0, x1, x2, normed, qkv, mixed, own, give, take,
           w0, wo0, wide, wide_o, mean_heads, ones, row_mask,
           sa1, sb1, ra1, rb1, sa2, sb2, ra2, rb2,
           ta1, tb1, ua1, ub1, ta2, tb2, ub2,
           local_sem, pair_sem, wsend, wrecv, ssem, rsem):
    frames, rows, width = x0.shape
    half = width // 2
    pairs = width // PAIR
    chunks = ra1.shape[0]
    band = rows // chunks
    count = frames * band
    tile = 2 * PAIR
    tok, s = lax.axis_index("tok"), lax.axis_index("sub")
    o = 1 - s
    gx, gy = tok // side, lax.rem(tok, side)
    slot_x, slot_y = gx * 2 + s, gy * 2 + s
    partner = {"sub": o}

    def other(g, k):
        return lax.rem(g + k, side)

    def at_x(g, core):
        return {"tok": g * side + gy, "sub": core}

    def at_y(g, core):
        return {"tok": gx * side + g, "sub": core}

    load_x = pltpu.make_async_copy(video_hbm, x0, local_sem.at[0])
    load_x.start()
    load_0 = [pltpu.make_async_copy(wqkv_hbm.at[0, part], w0.at[:, pl.ds(part * half, half)], local_sem.at[1 + part])
              for part in range(3)]
    load_0.append(pltpu.make_async_copy(wo_hbm.at[0], wo0, local_sem.at[4]))
    for copy in load_0:
        copy.start()
    mine = pl.multiple_of(s * half, half)

    def own_w(l):
        base = 5 + 4 * (l - 1)
        copies = [pltpu.make_async_copy(
            wqkv_hbm.at[l, part], wide.at[l - 1, :, pl.ds(part * width + mine, half)], local_sem.at[base + part])
            for part in range(3)]
        copies.append(pltpu.make_async_copy(wo_hbm.at[l], wide_o.at[l - 1, pl.ds(mine, half), :], local_sem.at[base + 3]))
        return copies

    def pass_w(l):
        copies = [pltpu.make_async_remote_copy(
            wqkv_hbm.at[l, part], wide.at[l - 1, :, pl.ds(part * width + mine, half)],
            wsend.at[l - 1, part], wrecv.at[l - 1, part], device_id=partner, device_id_type=MESH)
            for part in range(3)]
        copies.append(pltpu.make_async_remote_copy(
            wo_hbm.at[l], wide_o.at[l - 1, pl.ds(mine, half), :],
            wsend.at[l - 1, 3], wrecv.at[l - 1, 3], device_id=partner, device_id_type=MESH))
        return copies

    barrier = pltpu.get_barrier_semaphore()
    pl.semaphore_signal(barrier, inc=1, device_id=partner, device_id_type=MESH)
    for k in range(1, side):
        for core in range(2):
            pl.semaphore_signal(barrier, inc=1, device_id=at_x(other(gx, k), core), device_id_type=MESH)
            pl.semaphore_signal(barrier, inc=1, device_id=at_y(other(gy, k), core), device_id_type=MESH)
    for l in (1, 2):
        for copy in own_w(l):
            copy.start()

    i, j = iota((count, count), 0), iota((count, count), 1)
    two = 2 * side
    swap_lines = one_hot(j == lax.rem(i // 2, side) * two + (i // two) * 2 + lax.rem(i, 2))
    group = one_hot(j == lax.rem(i, side) * two + i // side)
    ungroup = one_hot(j == lax.rem(i, two) * side + i // two)
    swap_tokens = one_hot(j == lax.rem(i, side) * two + lax.rem(i // side, 2) * side + i // two)

    lane = iota((1, PAIR), 1)
    left, right = one_hot(lane < HEAD_DIM), one_hot(lane >= HEAD_DIM)
    r, c2 = iota((tile, tile), 0), iota((tile, tile), 1)
    mean_heads[...] = jnp.where(r // HEAD_DIM == c2 // HEAD_DIM, 1.0 / HEAD_DIM, 0.0).astype(BF16)
    i2, j2 = iota((count, 2 * count), 0), iota((count, 2 * count), 1)
    row_mask[...] = one_hot(lax.rem(i2, band) == lax.rem(j2, band))
    r, c2 = iota((2 * count, PAIR), 0), iota((2 * count, PAIR), 1)
    ones[...] = one_hot(r // count == c2 // HEAD_DIM)

    def span(c):
        return pl.ds(pl.multiple_of(c * band, band), band)

    def normalize(tokens, l):
        values = tokens.astype(F32)
        scale = lax.rsqrt(jnp.mean(values * values, axis=-1, keepdims=True) + EPSILON)
        return (values * scale * gain_ref[l:l + 1, :]).astype(BF16)

    def project(flat, w, total, scaled):
        every, tiles = matmul(flat, w[...]), []
        for start in range(0, total, tile):
            y = every[:, start:min(start + tile, total)]
            if start < scaled:
                y = y * lax.rsqrt(matmul((y * y).astype(BF16), mean_heads[...]) + EPSILON)
            tiles.append(y.astype(BF16))
        return tiles

    def pair_of(tiles, p):
        return tiles[p // 2][:, (p % 2) * PAIR:(p % 2 + 1) * PAIR]

    def attend(queries, keys, values, sums, mask):
        scores = [lax.dot_general(q, jnp.concatenate([k * left, k * right], axis=0), CROSS, preferred_element_type=F32)
                  for q, k in zip(queries, keys)]
        expos = [jnp.exp2(score * (math.log2(math.e) / math.sqrt(HEAD_DIM))).astype(BF16) for score in scores]
        if mask is not None:
            expos = [expo * mask for expo in expos]
        outs = []
        for expo, v in zip(expos, values):
            vv = jnp.concatenate([jnp.concatenate([v * left, v * right], axis=0), sums], axis=1)
            both = matmul(expo, vv)
            outs.append((both[:, :PAIR] / both[:, PAIR:]).astype(BF16))
        return jnp.concatenate(outs, axis=1)

    def attention(tiles, n, mask):
        split = [pair_of(tiles, p) for p in range(3 * n)]
        return attend(split[:n], split[n:2 * n], split[2 * n:], ones[...], mask)

    def permute(matrix, values):
        return matmul(matrix, values).astype(BF16)

    order = sorted(range(1, side), key=lambda k: -min(k, side - k))

    def ring(send, recv, sem, c, me, place):
        for k in order:
            g = other(me, k)
            pltpu.make_async_remote_copy(
                send.at[c, g], recv.at[c, me], ssem.at[sem, c], rsem.at[sem, c],
                device_id=place(g, s), device_id_type=MESH).start()
        recv[c, me] = send[c, me]

    def fan(send, recv, sem, c, me, slot, place):
        for k in order:
            g = other(me, k)
            for core in range(2):
                pltpu.make_async_remote_copy(
                    send.at[c, g * 2 + core], recv.at[c, slot], ssem.at[sem, c], rsem.at[sem, c],
                    device_id=place(g, core), device_id_type=MESH).start()
        pltpu.make_async_remote_copy(
            send.at[c, me * 2 + o], recv.at[c, slot], ssem.at[sem, c], rsem.at[sem, c],
            device_id=partner, device_id_type=MESH).start()
        recv[c, slot] = send[c, slot]

    def arrived(recv, sem, c):
        pieces = recv.at[c, pl.ds(0, recv.shape[1] - 1)]
        pltpu.make_async_copy(pieces, pieces, rsem.at[sem, c]).wait()

    def sent(send, sem, c):
        pieces = send.at[c, pl.ds(0, send.shape[1] - 1)]
        pltpu.make_async_copy(pieces, pieces, ssem.at[sem, c]).wait()

    def flat(recv, c):
        return recv[c].reshape(count, half)

    def start_out(c, values):
        sa1[c] = values[:, :half].reshape(side, two, half)
        sb1[c] = permute(swap_lines, values[:, half:]).reshape(side, two, half)
        ring(sa1, ra1, 0, c, gx, at_x)
        ring(sb1, rb1, 1, c, gy, at_y)

    def relay_out(c):
        arrived(ra1, 0, c)
        arrived(rb1, 1, c)
        sa2[c] = permute(group, flat(ra1, c)).reshape(two, side, half)
        sb2[c] = permute(group, flat(rb1, c)).reshape(two, side, half)
        fan(sa2, ra2, 2, c, gy, slot_y, at_y)
        fan(sb2, rb2, 3, c, gx, slot_x, at_x)

    def finish_out(c):
        arrived(ra2, 2, c)
        arrived(rb2, 3, c)
        return jnp.concatenate([flat(ra2, c), permute(swap_tokens, flat(rb2, c))], axis=1)

    def start_back(c, values):
        ta1[c] = values[:, :half].reshape(two, side, half)
        tb1[c] = permute(swap_tokens, values[:, half:]).reshape(two, side, half)
        fan(ta1, ua1, 4, c, gy, slot_y, at_y)
        fan(tb1, ub1, 5, c, gx, slot_x, at_x)

    def relay_back(c):
        arrived(ua1, 4, c)
        arrived(ub1, 5, c)
        tb2[c] = permute(ungroup, flat(ub1, c)).reshape(side, two, half)
        ta2[c] = permute(ungroup, flat(ua1, c)).reshape(side, two, half)
        for k in order:
            g = other(gx, k)
            pltpu.make_async_remote_copy(
                ta2.at[c, g], x2.at[gx, span(c), pl.ds(0, half)], ssem.at[6, c], rsem.at[6, c],
                device_id=at_x(g, s), device_id_type=MESH).start()
        x2[gx, span(c), 0:half] = ta2[c, gx]
        ring(tb2, ub2, 7, c, gy, at_y)

    def finish_back(c):
        sent_like = ta2.at[c, pl.ds(0, side - 1)]
        pltpu.make_async_copy(sent_like, sent_like, rsem.at[6, c]).wait()
        arrived(ub2, 7, c)
        x2[:, span(c), half:width] = permute(swap_lines, flat(ub2, c)).reshape(frames, band, half)

    def pass_normed(c):
        return pltpu.make_async_remote_copy(
            normed.at[0, :, span(c), :], normed.at[1, :, span(c), :], pair_sem.at[0, c], pair_sem.at[1, c],
            device_id=partner, device_id_type=MESH)

    def pass_update(c):
        return pltpu.make_async_remote_copy(
            give.at[c], take.at[c], pair_sem.at[2, c], pair_sem.at[3, c], device_id=partner, device_id_type=MESH)

    def heads(slot, c):
        tiles = project(normed[slot, :, span(c), :].reshape(count, width), w0, 3 * half, width)
        return matmul(attention(tiles, pairs // 2, row_mask[...]), wo0[...])

    load_x.wait()

    @pl.loop(0, chunks)
    def _(c):
        normed[0, :, span(c), :] = normalize(x0[:, span(c), :].reshape(count, width), 0).reshape(frames, band, width)

    for copy in load_0:
        copy.wait()

    @pl.loop(0, chunks)
    def _(c):
        own[c] = x0[:, span(c), :].reshape(count, width).astype(F32) + heads(0, c)

    pl.semaphore_wait(barrier, 4 * (side - 1) + 1)
    for c in range(chunks):
        pass_normed(c).start()

    @pl.loop(0, chunks)
    def _(c):
        pass_normed(c).wait_recv()
        give[c] = heads(1, c).astype(BF16)
        pass_update(c).start()

    @pl.loop(0, chunks)
    def _(c):
        pass_update(c).wait_recv()
        start_out(c, (own[c] + take[c].astype(F32)).astype(BF16))

    for copy in pass_w(1):
        copy.start()

    @pl.loop(0, chunks)
    def _(c):
        relay_out(c)

    for copy in pass_w(2):
        copy.start()

    for copy in own_w(1):
        copy.wait()
    for copy in pass_w(1):
        copy.wait_recv()

    @pl.loop(0, chunks)
    def _(c):
        line = finish_out(c)
        tiles = project(normalize(line, 1), wide.at[0], 3 * width, 2 * width)
        update = matmul(attention(tiles, pairs, None), wide_o[0])
        start_back(c, (line.astype(F32) + update).astype(BF16))

        @pl.when(c > 0)
        def _():
            relay_back(c - 1)

    def columns(c):
        finish_back(c)
        tiles = project(normalize(x2[:, span(c), :].reshape(count, width), 2), wide.at[1], 3 * width, 2 * width)
        for t, value in enumerate(tiles):
            part, at = divmod(t * tile, width)
            qkv[part, :, span(c), at:at + tile] = value.reshape(frames, band, tile)

    for copy in own_w(2):
        copy.wait()
    for copy in pass_w(2):
        copy.wait_recv()

    @pl.loop(0, chunks)
    def _(c):
        columns(c)

        @pl.when(c == 0)
        def _():
            relay_back(chunks - 1)

    sums = jnp.concatenate([jnp.broadcast_to(left, (rows, PAIR)), jnp.broadcast_to(right, (rows, PAIR))], axis=0)

    lanes = [slice(p * PAIR, (p + 1) * PAIR) for p in range(pairs)]

    @pl.loop(0, frames // 2)
    def _(f2):
        for f in (2 * f2, 2 * f2 + 1):
            mixed[f] = attend(*([qkv[part, f, :, at] for at in lanes] for part in range(3)), sums, None)

    @pl.loop(0, chunks)
    def _(c):
        total = x2[:, span(c), :].reshape(count, width).astype(F32) + matmul(
            mixed[:, span(c), :].reshape(count, width), wide_o[1])
        out_ref[:, span(c), :] = total.astype(BF16).reshape(frames, band, width)

    for l in (1, 2):
        for copy in pass_w(l):
            copy.wait_send()

    @pl.loop(0, chunks)
    def _(c):
        pass_normed(c).wait_send()
        pass_update(c).wait_send()
        for sem, send in enumerate((sa1, sb1, sa2, sb2, ta1, tb1, ta2, tb2)):
            sent(send, sem, c)


def body(side, video, norm_gain, qkv_weight, out_weight):
    frames, rows, cols, width = video.shape
    half = width // 2
    lines = 2 * side * side
    chunks = frames * rows // lines
    count = frames * rows // chunks
    ring = pltpu.VMEM((chunks, side, 2 * side, half), BF16)
    fan = pltpu.VMEM((chunks, 2 * side, side, half), BF16)
    tokens = pltpu.VMEM((frames, rows, width), BF16)
    dma = pltpu.SemaphoreType.DMA
    anywhere = pl.BlockSpec(memory_space=pltpu.HBM)
    vmem = pl.BlockSpec(memory_space=pltpu.VMEM)
    out = pl.pallas_call(
        functools.partial(kernel, side),
        out_shape=jax.ShapeDtypeStruct((frames, rows, width), BF16),
        in_specs=[anywhere, vmem, anywhere, anywhere],
        out_specs=vmem,
        scratch_shapes=[
            tokens, tokens, tokens,
            pltpu.VMEM((2, frames, rows, width), BF16),
            pltpu.VMEM((3, frames, rows, width), BF16),
            tokens,
            pltpu.VMEM((chunks, count, width), F32),
            pltpu.VMEM((chunks, count, width), BF16), pltpu.VMEM((chunks, count, width), BF16),
            pltpu.VMEM((width, 3 * half), BF16), pltpu.VMEM((half, width), BF16),
            pltpu.VMEM((2, width, 3 * width), BF16), pltpu.VMEM((2, width, width), BF16),
            pltpu.VMEM((2 * PAIR, 2 * PAIR), BF16), pltpu.VMEM((2 * count, PAIR), BF16),
            pltpu.VMEM((count, 2 * count), BF16),
            ring, ring, ring, ring, fan, fan, fan, fan,
            fan, fan, fan, fan, ring, ring, ring,
            dma((13,)), dma((4, chunks)), dma((2, 4)), dma((2, 4)), dma((8, chunks)), dma((8, chunks)),
        ],
        compiler_params=pltpu.CompilerParams(
            collective_id=0, has_side_effects=True, vmem_limit_bytes=50 * 1024 * 1024),
    )(*(pltpu.with_memory_space_constraint(a, pltpu.HBM) for a in (video.reshape(frames, rows, width), norm_gain, qkv_weight, out_weight)))
    return out.reshape(video.shape)


def solution(mesh):
    side = math.isqrt(mesh.shape["tok"])
    in_specs = (
        P("parts", None, ("tok", "sub"), None),
        P(),
        P(None, None, None, "sub"),
        P(None, "sub", None),
    )
    out_specs = P("parts", None, ("tok", "sub"), None)
    return jax.shard_map(functools.partial(body, side), mesh=mesh, in_specs=in_specs, out_specs=out_specs, check_vma=False)
```

time: 79.1 us -> 65.6 us (0.83)
  Pallas kernels: 76.9 us -> 64.6 us
  local copies, waits for them, and re-layouts: 1.92 us -> 0.82 us
    pallas_call x1, Pallas kernels: 76.9 us -> 64.6 us  [body(): pl.pallas_call(functools.partial(kernel, side), out_shape=jax.ShapeDtypeS...]
    unnamed x1, local copies, waits for them, and re-layouts: 1.92 us -> 0.82 us
where the time goes in v1:
time: 65.6 us; the launch traced here: 65.4 us
  Pallas kernels  64.6 us (98%)
  local copies, waits for them, and re-layouts  0.82 us (1%)
    pallas_call x1, Pallas kernels, body(): pl.pallas_call(functools.partial(kernel, side), out_shape=jax.ShapeDtypeS...  64.6 us

profile of v1, /device:TPU:513, one launch (start us, length us, event | category | flops | bytes accessed | tf_op | source)
XLA Modules:
  0.0 65.4 jit_solution(15328169722264183303)
XLA Ops:
  0.0 64.6 %shard_map.46 = bf16[8,48,768]{2,1,0:T(8,128)(2,1)S(1)} custom-call(bf16[8,48,768]{2,1,0:T(8,128)(2,1)} %bitcast.5, f32[3,768]{1,0:T(4,128)} %gain_ref.1, bf16[3,3,768,384]{3,2,1,0:T(8,128)(2,1)} %wqkv_hbm.1, bf16[3,384,768]{2,1,0:T(8,128)(2,1)} %wo_hbm.1), custom_call_target="tpu_custom_call" | custom-call | tf_op jit(solution)/shard_map/pallas_call | solution.py:355
  64.6 0.8 %copy.7 = bf16[8,48,1,768]{3,1,2,0:T(8,128)(2,1)} copy(bf16[8,48,1,768]{3,1,2,0:T(8,128)(2,1)S(1)} %bitcast.4) | data formatting | bytes 1179648

commit v2 on v1

v2 whole, which is shorter than its diff:
```python
import functools
import math

import jax
import jax.numpy as jnp
from jax import lax
from jax.experimental import pallas as pl
from jax.experimental.pallas import tpu as pltpu
from jax.sharding import PartitionSpec as P

HEAD_DIM = 64
EPSILON = 1e-06
PAIR = 2 * HEAD_DIM
MESH = pl.DeviceIdType.MESH
F32, BF16 = jnp.float32, jnp.bfloat16
CROSS = (((1,), (1,)), ((), ()))


def iota(shape, dim):
    return lax.broadcasted_iota(jnp.int32, shape, dim)


def one_hot(condition):
    return jnp.where(condition, 1.0, 0.0).astype(BF16)


def matmul(a, b):
    return jnp.dot(a, b, preferred_element_type=F32)


def kernel(side, video_hbm, gain_ref, wqkv_hbm, wo_hbm, out_ref,
           x0, x2, normed, qkv, mixed, own, give, take,
           w0, wo0, wide, wide_o, mean_heads, ones, row_mask,
           out1, in1, out2, in2, back1, land1, back2,
           local_sem, pair_sem, wsend, wrecv, ssem, rsem):
    frames, rows, width = x0.shape
    half = width // 2
    pairs = width // PAIR
    chunks = in1.shape[0]
    band = rows // chunks
    count = frames * band
    tile = 2 * PAIR
    tok, s = lax.axis_index("tok"), lax.axis_index("sub")
    o = 1 - s
    gx, gy = tok // side, lax.rem(tok, side)
    last = gx * s + gy * o
    last_o = gx * o + gy * s
    partner = {"sub": o}

    def other(g, k):
        return lax.rem(g + k, side)

    def at_x(g, core):
        return {"tok": g * side + gy, "sub": core}

    def at_y(g, core):
        return {"tok": gx * side + g, "sub": core}

    order = sorted(range(1, side), key=lambda k: -min(k, side - k))
    load_x = pltpu.make_async_copy(video_hbm, x0, local_sem.at[0])
    load_x.start()
    barrier = pltpu.get_barrier_semaphore()
    pl.semaphore_signal(barrier, inc=1, device_id=partner, device_id_type=MESH)
    for k in order:
        for core in range(2):
            pl.semaphore_signal(barrier, inc=1, device_id=at_x(other(gx, k), core), device_id_type=MESH)
            pl.semaphore_signal(barrier, inc=1, device_id=at_y(other(gy, k), core), device_id_type=MESH)
    load_0 = [pltpu.make_async_copy(wqkv_hbm.at[0, part], w0.at[:, pl.ds(part * half, half)], local_sem.at[1 + part])
              for part in range(3)]
    load_0.append(pltpu.make_async_copy(wo_hbm.at[0], wo0, local_sem.at[4]))
    for copy in load_0:
        copy.start()
    mine = pl.multiple_of(s * half, half)

    def own_w(l):
        base = 5 + 4 * (l - 1)
        copies = [pltpu.make_async_copy(
            wqkv_hbm.at[l, part], wide.at[l - 1, :, pl.ds(part * width + mine, half)], local_sem.at[base + part])
            for part in range(3)]
        copies.append(pltpu.make_async_copy(wo_hbm.at[l], wide_o.at[l - 1, pl.ds(mine, half), :], local_sem.at[base + 3]))
        return copies

    def pass_w(l):
        copies = [pltpu.make_async_remote_copy(
            wqkv_hbm.at[l, part], wide.at[l - 1, :, pl.ds(part * width + mine, half)],
            wsend.at[l - 1, part], wrecv.at[l - 1, part], device_id=partner, device_id_type=MESH)
            for part in range(3)]
        copies.append(pltpu.make_async_remote_copy(
            wo_hbm.at[l], wide_o.at[l - 1, pl.ds(mine, half), :],
            wsend.at[l - 1, 3], wrecv.at[l - 1, 3], device_id=partner, device_id_type=MESH))
        return copies

    for l in (1, 2):
        for copy in own_w(l):
            copy.start()

    i, j = iota((count, count), 0), iota((count, count), 1)
    square = side * side
    turn = one_hot(j == (i // square) * square + lax.rem(i, side) * side + lax.rem(i, square) // side)

    lane = iota((1, PAIR), 1)
    left, right = one_hot(lane < HEAD_DIM), one_hot(lane >= HEAD_DIM)
    r, c2 = iota((tile, tile), 0), iota((tile, tile), 1)
    mean_heads[...] = jnp.where(r // HEAD_DIM == c2 // HEAD_DIM, 1.0 / HEAD_DIM, 0.0).astype(BF16)
    i2, j2 = iota((count, 2 * count), 0), iota((count, 2 * count), 1)
    row_mask[...] = one_hot(lax.rem(i2, band) == lax.rem(j2, band))
    r, c2 = iota((2 * count, PAIR), 0), iota((2 * count, PAIR), 1)
    ones[...] = one_hot(r // count == c2 // HEAD_DIM)

    def span(c):
        return pl.ds(pl.multiple_of(c * band, band), band)

    def normalize(tokens, l):
        values = tokens.astype(F32)
        scale = lax.rsqrt(jnp.mean(values * values, axis=-1, keepdims=True) + EPSILON)
        return (values * scale * gain_ref[l:l + 1, :]).astype(BF16)

    def project(flat, w, total, scaled):
        every, tiles = matmul(flat, w[...]), []
        for start in range(0, total, tile):
            y = every[:, start:min(start + tile, total)]
            if start < scaled:
                y = y * lax.rsqrt(matmul((y * y).astype(BF16), mean_heads[...]) + EPSILON)
            tiles.append(y.astype(BF16))
        return tiles

    def pair_of(tiles, p):
        return tiles[p // 2][:, (p % 2) * PAIR:(p % 2 + 1) * PAIR]

    def attend(queries, keys, values, sums, mask):
        scores = [lax.dot_general(q, jnp.concatenate([k * left, k * right], axis=0), CROSS, preferred_element_type=F32)
                  for q, k in zip(queries, keys)]
        expos = [jnp.exp2(score * (math.log2(math.e) / math.sqrt(HEAD_DIM))).astype(BF16) for score in scores]
        if mask is not None:
            expos = [expo * mask for expo in expos]
        outs = []
        for expo, v in zip(expos, values):
            vv = jnp.concatenate([jnp.concatenate([v * left, v * right], axis=0), sums], axis=1)
            both = matmul(expo, vv)
            outs.append((both[:, :PAIR] / both[:, PAIR:]).astype(BF16))
        return jnp.concatenate(outs, axis=1)

    def attention(tiles, n, mask):
        split = [pair_of(tiles, p) for p in range(3 * n)]
        return attend(split[:n], split[n:2 * n], split[2 * n:], ones[...], mask)

    def permute(matrix, values):
        return matmul(matrix, values).astype(BF16)

    def push(src, dst, sem, c, device):
        pltpu.make_async_remote_copy(src, dst, ssem.at[sem, c], rsem.at[sem, c], device_id=device, device_id_type=MESH).start()

    def arrived(ref, sem, c):
        pltpu.make_async_copy(ref, ref, rsem.at[sem, c]).wait()

    def sent(ref, sem, c):
        pltpu.make_async_copy(ref, ref, ssem.at[sem, c]).wait()

    def all_but(ref, c, n):
        return ref.at[c, pl.ds(0, n)]

    def turned(ref, c):
        return permute(turn, ref[c].reshape(count, width)).reshape(2 * side, side, width)

    def start_out(c, values):
        out1[c] = values.reshape(2 * side, side, width)
        for k in order:
            x, y = other(gx, k), other(gy, k)
            push(out1.at[c, x * 2], in1.at[c, gx], 0, c, at_x(x, s))
            push(out1.at[c, y * 2 + 1], in1.at[c, side + gy], 0, c, at_y(y, s))
        in1[c, gx] = out1[c, gx * 2]
        in1[c, side + gy] = out1[c, gy * 2 + 1]

    def relay_out(c):
        arrived(all_but(in1, c, 2 * side - 2), 0, c)
        out2[c] = turned(in1, c)
        for k in order:
            x, y = other(gx, k), other(gy, k)
            push(out2.at[c, y], in2.at[c, gy * 2 + s], 1, c, at_y(y, 0))
            push(out2.at[c, side + x], in2.at[c, gx * 2 + s], 1, c, at_x(x, 1))
        push(out2.at[c, o * side + last_o], in2.at[c, last_o * 2 + s], 1, c, partner)
        in2[c, last * 2 + s] = out2[c, s * side + last]

    def start_back(c, values):
        back1[c] = values.reshape(2 * side, side, width)
        for k in order:
            g = other(last, k)
            chip = s * (g * side + gy) + o * (gx * side + g)
            for core in range(2):
                push(back1.at[c, g * 2 + core], land1.at[c, s * side + last], 2, c, {"tok": chip, "sub": core})
        push(back1.at[c, last * 2 + o], land1.at[c, s * side + last], 2, c, partner)
        land1[c, s * side + last] = back1[c, last * 2 + s]

    def relay_back(c):
        arrived(all_but(land1, c, 2 * side - 1), 2, c)
        back2[c] = turned(land1, c)
        for k in order:
            x, y = other(gx, k), other(gy, k)
            push(back2.at[c, x], x2.at[gx, c, 0], 3, c, at_x(x, s))
            push(back2.at[c, side + y], x2.at[gy, c, 1], 3, c, at_y(y, s))
        x2[gx, c, 0] = back2[c, gx]
        x2[gy, c, 1] = back2[c, side + gy]

    def finish_back(c):
        arrived(all_but(back2, c, 2 * side - 2), 3, c)

    def pass_normed(c):
        return pltpu.make_async_remote_copy(
            normed.at[0, :, span(c), :], normed.at[1, :, span(c), :], pair_sem.at[0, c], pair_sem.at[1, c],
            device_id=partner, device_id_type=MESH)

    def pass_update(c):
        return pltpu.make_async_remote_copy(
            give.at[:, span(c), :], take.at[:, span(c), :], pair_sem.at[2, c], pair_sem.at[3, c],
            device_id=partner, device_id_type=MESH)

    def project_heads(slot):
        tiles = project(normed[slot].reshape(frames * rows, width), w0, 3 * half, width)
        for part in range(3):
            for p in range(pairs // 2):
                qkv[part, :, :, p * PAIR:(p + 1) * PAIR] = pair_of(tiles, part * (pairs // 2) + p).reshape(frames, rows, PAIR)

    def attend_heads():
        for c in range(chunks):
            at = slice(c * band, (c + 1) * band)
            split = [[qkv[part, :, at, p * PAIR:(p + 1) * PAIR].reshape(count, PAIR) for p in range(pairs // 2)]
                     for part in range(3)]
            mixed[:, at, 0:half] = attend(*split, ones[...], row_mask[...]).reshape(frames, band, half)
        return matmul(mixed[:, :, 0:half].reshape(frames * rows, half), wo0[...])

    load_x.wait()

    @pl.loop(0, chunks)
    def _(c):
        normed[0, :, span(c), :] = normalize(x0[:, span(c), :].reshape(count, width), 0).reshape(frames, band, width)

    for copy in load_0:
        copy.wait()

    project_heads(0)
    pl.semaphore_wait(barrier, 4 * (side - 1) + 1)
    for c in range(chunks):
        pass_normed(c).start()
    own[...] = x0[...].astype(F32) + attend_heads().reshape(frames, rows, width)

    def join(c):
        pass_update(c).wait_recv()
        at = slice(c * band, (c + 1) * band)
        start_out(c, (own[:, at, :] + take[:, at, :].astype(F32)).astype(BF16).reshape(count, width))

    for c in range(chunks):
        pass_normed(c).wait_recv()
        tiles = project(normed[1, :, c * band:(c + 1) * band, :].reshape(count, width), w0, 3 * half, width)
        update = matmul(attention(tiles, pairs // 2, row_mask[...]), wo0[...])
        give[:, c * band:(c + 1) * band, :] = update.astype(BF16).reshape(frames, band, width)
        pass_update(c).start()
        if c > 0:
            join(c - 1)
    join(chunks - 1)

    for copy in pass_w(1):
        copy.start()

    @pl.loop(0, chunks)
    def _(c):
        relay_out(c)

    for copy in pass_w(2):
        copy.start()

    for copy in own_w(1):
        copy.wait()
    for copy in pass_w(1):
        copy.wait_recv()

    @pl.loop(0, chunks)
    def _(c):
        arrived(all_but(in2, c, 2 * side - 1), 1, c)
        line = in2[c].reshape(count, width)
        tiles = project(normalize(line, 1), wide.at[0], 3 * width, 2 * width)
        update = matmul(attention(tiles, pairs, None), wide_o[0])
        start_back(c, (line.astype(F32) + update).astype(BF16))

    @pl.loop(0, chunks)
    def _(c):
        relay_back(c)

    def columns(c):
        finish_back(c)
        tiles = project(normalize(x2[:, c].reshape(count, width), 2), wide.at[1], 3 * width, 2 * width)
        for t, value in enumerate(tiles):
            part, at = divmod(t * tile, width)
            qkv[part, :, span(c), at:at + tile] = value.reshape(frames, band, tile)

    for copy in own_w(2):
        copy.wait()
    for copy in pass_w(2):
        copy.wait_recv()

    @pl.loop(0, chunks)
    def _(c):
        columns(c)

    sums = jnp.concatenate([jnp.broadcast_to(left, (rows, PAIR)), jnp.broadcast_to(right, (rows, PAIR))], axis=0)

    lanes = [slice(p * PAIR, (p + 1) * PAIR) for p in range(pairs)]

    @pl.loop(0, frames // 2)
    def _(f2):
        for f in (2 * f2, 2 * f2 + 1):
            mixed[f] = attend(*([qkv[part, f, :, at] for at in lanes] for part in range(3)), sums, None)

    total = x2[...].reshape(frames * rows, width).astype(F32) + matmul(mixed[...].reshape(frames * rows, width), wide_o[1])
    out_ref[...] = total.astype(BF16).reshape(frames, rows, width)

    for l in (1, 2):
        for copy in pass_w(l):
            copy.wait_send()

    @pl.loop(0, chunks)
    def _(c):
        pass_normed(c).wait_send()
        pass_update(c).wait_send()
        for sem, (ref, n) in enumerate(((out1, 2), (out2, 1), (back1, 1), (back2, 2))):
            sent(all_but(ref, c, 2 * side - n), sem, c)


def body(side, video, norm_gain, qkv_weight, out_weight):
    frames, rows, cols, width = video.shape
    half = width // 2
    lines = 2 * side * side
    chunks = frames * rows // lines
    count = frames * rows // chunks
    blocks = pltpu.VMEM((chunks, 2 * side, side, width), BF16)
    tokens = pltpu.VMEM((frames, rows, width), BF16)
    dma = pltpu.SemaphoreType.DMA
    anywhere = pl.BlockSpec(memory_space=pltpu.HBM)
    vmem = pl.BlockSpec(memory_space=pltpu.VMEM)
    out = pl.pallas_call(
        functools.partial(kernel, side),
        out_shape=jax.ShapeDtypeStruct((frames, rows, width), BF16),
        in_specs=[anywhere, vmem, anywhere, anywhere],
        out_specs=vmem,
        scratch_shapes=[
            tokens,
            pltpu.VMEM((frames, chunks, 2, side, width), BF16),
            pltpu.VMEM((2, frames, rows, width), BF16),
            pltpu.VMEM((3, frames, rows, width), BF16),
            tokens,
            pltpu.VMEM((frames, rows, width), F32), tokens, tokens,
            pltpu.VMEM((width, 3 * half), BF16), pltpu.VMEM((half, width), BF16),
            pltpu.VMEM((2, width, 3 * width), BF16), pltpu.VMEM((2, width, width), BF16),
            pltpu.VMEM((2 * PAIR, 2 * PAIR), BF16), pltpu.VMEM((2 * count, PAIR), BF16),
            pltpu.VMEM((count, 2 * count), BF16),
            blocks, blocks, blocks, blocks, blocks, blocks, blocks,
            dma((13,)), dma((4, chunks)), dma((2, 4)), dma((2, 4)), dma((4, chunks)), dma((4, chunks)),
        ],
        compiler_params=pltpu.CompilerParams(
            collective_id=0, has_side_effects=True, vmem_limit_bytes=50 * 1024 * 1024),
    )(*(pltpu.with_memory_space_constraint(a, pltpu.HBM) for a in (video.reshape(frames, rows, width), norm_gain, qkv_weight, out_weight)))
    return out.reshape(video.shape)


def solution(mesh):
    side = math.isqrt(mesh.shape["tok"])
    in_specs = (
        P("parts", None, ("tok", "sub"), None),
        P(),
        P(None, None, None, "sub"),
        P(None, "sub", None),
    )
    out_specs = P("parts", None, ("tok", "sub"), None)
    return jax.shard_map(functools.partial(body, side), mesh=mesh, in_specs=in_specs, out_specs=out_specs, check_vma=False)
```

time: 65.6 us -> 62.2 us (0.948)
  Pallas kernels: 64.6 us -> 61.2 us
    pallas_call x1, Pallas kernels: 64.6 us -> 61.2 us  [body(): pl.pallas_call(functools.partial(kernel, side), out_shape=jax.ShapeDtypeS...]
where the time goes in v2:
time: 62.2 us; the launch traced here: 62 us
  Pallas kernels  61.2 us (98%)
  local copies, waits for them, and re-layouts  0.82 us (1%)
    pallas_call x1, Pallas kernels, body(): pl.pallas_call(functools.partial(kernel, side), out_shape=jax.ShapeDtypeS...  61.2 us

profile of v2, /device:TPU:513, one launch (start us, length us, event | category | flops | bytes accessed | tf_op | source)
XLA Modules:
  0.0 62.0 jit_solution(9512985753220576523)
XLA Ops:
  0.0 61.2 %shard_map.46 = bf16[8,48,768]{2,1,0:T(8,128)(2,1)S(1)} custom-call(bf16[8,48,768]{2,1,0:T(8,128)(2,1)} %bitcast.5, f32[3,768]{1,0:T(4,128)} %gain_ref.1, bf16[3,3,768,384]{3,2,1,0:T(8,128)(2,1)} %wqkv_hbm.1, bf16[3,384,768]{2,1,0:T(8,128)(2,1)} %wo_hbm.1), custom_call_target="tpu_custom_call" | custom-call | tf_op jit(solution)/shard_map/pallas_call | solution.py:339
  61.2 0.8 %copy.7 = bf16[8,48,1,768]{3,1,2,0:T(8,128)(2,1)} copy(bf16[8,48,1,768]{3,1,2,0:T(8,128)(2,1)S(1)} %bitcast.4) | data formatting | bytes 1179648

commit v3 on v2

--- a/solution.py
+++ b/solution.py
@@ -124,6 +124,20 @@
             tiles.append(y.astype(BF16))
         return tiles
 
+    def project_tokens(tokens, l, w):
+        values = tokens.astype(F32)
+        every = matmul((values * gain_ref[l:l + 1, :]).astype(BF16), w[...])
+        spread = jnp.mean(values * values, axis=-1, keepdims=True) + EPSILON
+        tiles = []
+        for start in range(0, 3 * width, tile):
+            y = every[:, start:start + tile]
+            if start < 2 * width:
+                y = y * lax.rsqrt(matmul((y * y).astype(BF16), mean_heads[...]) + EPSILON * spread)
+            else:
+                y = y * lax.rsqrt(spread)
+            tiles.append(y.astype(BF16))
+        return tiles
+
     def pair_of(tiles, p):
         return tiles[p // 2][:, (p % 2) * PAIR:(p % 2 + 1) * PAIR]
 
@@ -203,6 +217,7 @@
 
     def finish_back(c):
         arrived(all_but(back2, c, 2 * side - 2), 3, c)
+        sent(all_but(back2, c, 2 * side - 2), 3, c)
 
     def pass_normed(c):
         return pltpu.make_async_remote_copy(
@@ -277,7 +292,7 @@
     def _(c):
         arrived(all_but(in2, c, 2 * side - 1), 1, c)
         line = in2[c].reshape(count, width)
-        tiles = project(normalize(line, 1), wide.at[0], 3 * width, 2 * width)
+        tiles = project_tokens(line, 1, wide.at[0])
         update = matmul(attention(tiles, pairs, None), wide_o[0])
         start_back(c, (line.astype(F32) + update).astype(BF16))
 
@@ -285,9 +300,20 @@
     def _(c):
         relay_back(c)
 
+    for l in (1, 2):
+        for copy in pass_w(l):
+            copy.wait_send()
+
+    @pl.loop(0, chunks)
+    def _(c):
+        pass_normed(c).wait_send()
+        pass_update(c).wait_send()
+        for sem, (ref, n) in enumerate(((out1, 2), (out2, 1), (back1, 1))):
+            sent(all_but(ref, c, 2 * side - n), sem, c)
+
     def columns(c):
         finish_back(c)
-        tiles = project(normalize(x2[:, c].reshape(count, width), 2), wide.at[1], 3 * width, 2 * width)
+        tiles = project_tokens(x2[:, c].reshape(count, width), 2, wide.at[1])
         for t, value in enumerate(tiles):
             part, at = divmod(t * tile, width)
             qkv[part, :, span(c), at:at + tile] = value.reshape(frames, band, tile)
@@ -305,24 +331,13 @@
 
     lanes = [slice(p * PAIR, (p + 1) * PAIR) for p in range(pairs)]
 
-    @pl.loop(0, frames // 2)
-    def _(f2):
-        for f in (2 * f2, 2 * f2 + 1):
+    @pl.loop(0, frames // 4)
+    def _(f4):
+        for f in (4 * f4, 4 * f4 + 1, 4 * f4 + 2, 4 * f4 + 3):
             mixed[f] = attend(*([qkv[part, f, :, at] for at in lanes] for part in range(3)), sums, None)
 
     total = x2[...].reshape(frames * rows, width).astype(F32) + matmul(mixed[...].reshape(frames * rows, width), wide_o[1])
     out_ref[...] = total.astype(BF16).reshape(frames, rows, width)
-
-    for l in (1, 2):
-        for copy in pass_w(l):
-            copy.wait_send()
-
-    @pl.loop(0, chunks)
-    def _(c):
-        pass_normed(c).wait_send()
-        pass_update(c).wait_send()
-        for sem, (ref, n) in enumerate(((out1, 2), (out2, 1), (back1, 1), (back2, 2))):
-            sent(all_but(ref, c, 2 * side - n), sem, c)
 
 
 def body(side, video, norm_gain, qkv_weight, out_weight):

time: 62.2 us -> 61.7 us (level)
  no operation moved by 1% of the time
where the time goes in v3:
time: 61.7 us; the launch traced here: 61.6 us
  Pallas kernels  60.7 us (98%)
  local copies, waits for them, and re-layouts  0.82 us (1%)
    pallas_call x1, Pallas kernels, body(): pl.pallas_call(functools.partial(kernel, side), out_shape=jax.ShapeDtypeS...  60.7 us

profile of v3, /device:TPU:513, one launch (start us, length us, event | category | flops | bytes accessed | tf_op | source)
XLA Modules:
  0.0 61.6 jit_solution(13539716701943935813)
XLA Ops:
  0.0 60.7 %shard_map.46 = bf16[8,48,768]{2,1,0:T(8,128)(2,1)S(1)} custom-call(bf16[8,48,768]{2,1,0:T(8,128)(2,1)} %bitcast.5, f32[3,768]{1,0:T(4,128)} %gain_ref.1, bf16[3,3,768,384]{3,2,1,0:T(8,128)(2,1)} %wqkv_hbm.1, bf16[3,384,768]{2,1,0:T(8,128)(2,1)} %wo_hbm.1), custom_call_target="tpu_custom_call" | custom-call | tf_op jit(solution)/shard_map/pallas_call | solution.py:354
  60.7 0.8 %copy.7 = bf16[8,48,1,768]{3,1,2,0:T(8,128)(2,1)} copy(bf16[8,48,1,768]{3,1,2,0:T(8,128)(2,1)S(1)} %bitcast.4) | data formatting | bytes 1179648

commit v4 on v3

--- a/solution.py
+++ b/solution.py
@@ -28,7 +28,7 @@
     return jnp.dot(a, b, preferred_element_type=F32)
 
 
-def kernel(side, video_hbm, gain_ref, wqkv_hbm, wo_hbm, out_ref,
+def kernel(side, video_hbm, gain_hbm, wqkv_hbm, wo_hbm, out_ref, gain_ref,
            x0, x2, normed, qkv, mixed, own, give, take,
            w0, wo0, wide, wide_o, mean_heads, ones, row_mask,
            out1, in1, out2, in2, back1, land1, back2,
@@ -59,6 +59,8 @@
     order = sorted(range(1, side), key=lambda k: -min(k, side - k))
     load_x = pltpu.make_async_copy(video_hbm, x0, local_sem.at[0])
     load_x.start()
+    load_gain = pltpu.make_async_copy(gain_hbm, gain_ref, local_sem.at[13])
+    load_gain.start()
     barrier = pltpu.get_barrier_semaphore()
     pl.semaphore_signal(barrier, inc=1, device_id=partner, device_id_type=MESH)
     for k in order:
@@ -244,6 +246,7 @@
         return matmul(mixed[:, :, 0:half].reshape(frames * rows, half), wo0[...])
 
     load_x.wait()
+    load_gain.wait()
 
     @pl.loop(0, chunks)
     def _(c):
@@ -354,9 +357,10 @@
     out = pl.pallas_call(
         functools.partial(kernel, side),
         out_shape=jax.ShapeDtypeStruct((frames, rows, width), BF16),
-        in_specs=[anywhere, vmem, anywhere, anywhere],
+        in_specs=[anywhere, anywhere, anywhere, anywhere],
         out_specs=vmem,
         scratch_shapes=[
+            pltpu.VMEM(norm_gain.shape, F32),
             tokens,
             pltpu.VMEM((frames, chunks, 2, side, width), BF16),
             pltpu.VMEM((2, frames, rows, width), BF16),
@@ -368,7 +372,7 @@
             pltpu.VMEM((2 * PAIR, 2 * PAIR), BF16), pltpu.VMEM((2 * count, PAIR), BF16),
             pltpu.VMEM((count, 2 * count), BF16),
             blocks, blocks, blocks, blocks, blocks, blocks, blocks,
-            dma((13,)), dma((4, chunks)), dma((2, 4)), dma((2, 4)), dma((4, chunks)), dma((4, chunks)),
+            dma((14,)), dma((4, chunks)), dma((2, 4)), dma((2, 4)), dma((4, chunks)), dma((4, chunks)),
         ],
         compiler_params=pltpu.CompilerParams(
             collective_id=0, has_side_effects=True, vmem_limit_bytes=50 * 1024 * 1024),

time: 61.7 us -> 61 us (0.989)
  Pallas kernels: 60.7 us -> 60 us
    pallas_call x1, Pallas kernels: 60.7 us -> 60 us  [body(): pl.pallas_call(functools.partial(kernel, side), out_shape=jax.ShapeDtypeS...]
where the time goes in v4:
time: 61 us; the launch traced here: 60.9 us
  Pallas kernels  60 us (98%)
  local copies, waits for them, and re-layouts  0.82 us (1%)
    pallas_call x1, Pallas kernels, body(): pl.pallas_call(functools.partial(kernel, side), out_shape=jax.ShapeDtypeS...  60 us

profile of v4, /device:TPU:513, one launch (start us, length us, event | category | flops | bytes accessed | tf_op | source)
XLA Modules:
  0.0 60.9 jit_solution(603339697994478464)
XLA Ops:
  0.0 60.0 %shard_map.46 = bf16[8,48,768]{2,1,0:T(8,128)(2,1)S(1)} custom-call(bf16[8,48,768]{2,1,0:T(8,128)(2,1)} %bitcast.5, f32[3,768]{1,0:T(4,128)} %gain_hbm.1, bf16[3,3,768,384]{3,2,1,0:T(8,128)(2,1)} %wqkv_hbm.1, bf16[3,384,768]{2,1,0:T(8,128)(2,1)} %wo_hbm.1), custom_call_target="tpu_custom_call" | custom-call | tf_op jit(solution)/shard_map/pallas_call | solution.py:357
  60.0 0.8 %copy.7 = bf16[8,48,1,768]{3,1,2,0:T(8,128)(2,1)} copy(bf16[8,48,1,768]{3,1,2,0:T(8,128)(2,1)S(1)} %bitcast.4) | data formatting | bytes 1179648
